TPU v7x, 32 devices: a whole 2x2x4 slice. The times are simulated.
32 devices in a mesh: groups: 2 (over y), seq: 4 (over z), head: 4 (over x, core).
Axes of the slice: x: 2, y: 2, z: 4, core: 2. Of those that a mesh axis runs over, the one named last changes fastest.
Arguments:
- queries: bfloat16 [2048, 8192], P(('groups', 'seq'), 'head'), parts along dimension 0, may hold values from -16 to 16
- keys: bfloat16 [2048, 1024], P(('groups', 'seq'), 'head'), parts along dimension 0, may hold values from -16 to 16
- values: bfloat16 [2048, 1024], P(('groups', 'seq'), 'head'), parts along dimension 0, may hold values from -6 to 6
- prompt_len: int32 [2], P('groups'), parts along dimension 0, may hold values from 256 to 1024
- page_dest: int32 [8, 2], P('groups'), parts along dimension 0, may hold values from 0 to 3, all different within a row; in each aligned block of 4 rows (0 to 3, 4 to 7, ...) at most 4 rows name the same one
Outputs:
- attended: bfloat16 [2048, 8192], P(('groups', 'seq'), 'head'), parts along dimension 0
- decode_page_cache: bfloat16 [32, 128, 2048], P(('groups', 'seq'), None, 'head'), parts along dimension 0
There are 2 independent parts, one for each index of `groups`. A program takes and returns all parts, laid end to end along the dimension named above; each array names one. Nothing has to cross between parts.
Inputs may be any that keep to these rules, and one draw needn't show every extreme that they name: `page_dest`: row s names the decode devices of the 2 pages of tokens s * 256 to (s + 1) * 256 - 1, all different within a row; no device is named more than 4 times in all, and some device exactly 4 times.
All inputs are finite; a program needn't handle non-finite values.
Results may differ from a plain program's by a relative error of at most 0.005.
Values may be sent and summed in bfloat16 or wider, within the bound.
A program may use at most 64 MiB of HBM per device.

v0:
```python
import math
import jax
import jax.numpy as jnp
from jax import lax
from jax.sharding import PartitionSpec as P

HEAD_SIZE = 128
PAGE_TOKENS = 128
NEG_FILL = -1e30


def blank_state(kv_heads, group_size, query_count):
    return (
        jnp.full((kv_heads, group_size, query_count), NEG_FILL, jnp.float32),
        jnp.zeros((kv_heads, group_size, query_count), jnp.float32),
        jnp.zeros((kv_heads, group_size, query_count, HEAD_SIZE), jnp.float32),
    )


def attend_block(
    query_state, query_block, query_pos, key_block, value_block, block_start, prompt_end
):
    key_count = key_block.shape[0]
    kv_heads = key_block.shape[1] // HEAD_SIZE
    keys_split = key_block.reshape(key_count, kv_heads, HEAD_SIZE)
    values_split = value_block.reshape(key_count, kv_heads, HEAD_SIZE)
    scores = jnp.einsum(
        "rkgd,pkd->kgrp", query_block, keys_split, preferred_element_type=jnp.float32
    )
    scores = scores * (1.0 / math.sqrt(HEAD_SIZE))
    key_pos = block_start + jnp.arange(key_count, dtype=jnp.int32)
    allowed = (key_pos[None, :] <= query_pos[:, None]) & (key_pos[None, :] < prompt_end)
    scores = jnp.where(allowed, scores, NEG_FILL)
    old_max = query_state[0]
    new_max = jnp.maximum(old_max, jnp.max(scores, axis=-1))
    weights = jnp.where(allowed, jnp.exp(scores - new_max[..., None]), 0.0)
    factor = jnp.exp(old_max - new_max)
    denominator = query_state[1] * factor + jnp.sum(weights, axis=-1)
    accumulated = query_state[2] * factor[..., None] + jnp.einsum(
        "kgrp,pkd->kgrd",
        weights.astype(jnp.bfloat16),
        values_split,
        preferred_element_type=jnp.float32,
    )
    return (new_max, denominator, accumulated)


def finish(query_state, query_pos, prompt_end):
    query_live = query_pos < prompt_end
    safe_total = jnp.where(query_live[None, None, :], query_state[1], 1.0)
    result = jnp.where(query_live[None, None, :, None], query_state[2] / safe_total[..., None], 0.0)
    query_count = query_pos.shape[0]
    return result.transpose(2, 0, 1, 3).reshape(query_count, -1).astype(jnp.bfloat16)


def join_pages(key_rows, value_rows):
    page_count = key_rows.shape[0] // PAGE_TOKENS
    kv_heads = key_rows.shape[1] // HEAD_SIZE
    stacked = jnp.stack(
        (
            key_rows.reshape(page_count, PAGE_TOKENS, kv_heads, HEAD_SIZE),
            value_rows.reshape(page_count, PAGE_TOKENS, kv_heads, HEAD_SIZE),
        ),
        axis=3,
    )
    return stacked.reshape(page_count, PAGE_TOKENS, 2 * key_rows.shape[1])


def slot_pages(page_dest, owner, slots):
    flat_dest = page_dest.reshape(-1)
    page_order = jnp.arange(flat_dest.shape[0], dtype=jnp.int32)
    same_dest = flat_dest[:, None] == flat_dest[None, :]
    dest_rank = jnp.sum(same_dest & (page_order[None, :] < page_order[:, None]), axis=1)
    matched = (flat_dest[:, None] == owner) & (
        dest_rank[:, None] == jnp.arange(slots, dtype=jnp.int32)[None, :]
    )
    page_index = jnp.sum(jnp.where(matched, page_order[:, None], 0), axis=0)
    present = jnp.any(matched, axis=0)
    return (flat_dest, page_index, present)


def place_pages(stored, key_block, value_block, block_start, prompt_end, page_index, present):
    key_pos = block_start + jnp.arange(key_block.shape[0], dtype=jnp.int32)
    token_present = (key_pos < prompt_end)[:, None]
    block_pages = join_pages(
        jnp.where(token_present, key_block, 0), jnp.where(token_present, value_block, 0)
    )
    page_count = block_pages.shape[0]
    local_index = page_index - block_start // PAGE_TOKENS
    inside = present & (local_index >= 0) & (local_index < page_count)
    picked = block_pages[jnp.clip(local_index, 0, page_count - 1)]
    return jnp.where(inside[:, None, None], picked, stored)


def local(queries, keys, values, prompt_len, page_dest):
    shard_rows = queries.shape[0]
    kv_width = keys.shape[1]
    kv_heads = kv_width // HEAD_SIZE
    group_size = queries.shape[1] // kv_width
    seq_index = lax.axis_index("seq")
    prompt_end = prompt_len[0]
    per_device = page_dest.shape[1]
    slots = 2 * per_device
    flat_dest, page_index, present = slot_pages(page_dest, seq_index, slots)
    own_rows = seq_index * shard_rows + jnp.arange(shard_rows, dtype=jnp.int32)
    query_parts = (queries,)
    positions = (own_rows,)
    shaped = tuple(
        (
            part_rows.reshape(part_rows.shape[0], kv_heads, group_size, HEAD_SIZE)
            for part_rows in query_parts
        )
    )
    states = tuple(
        (blank_state(kv_heads, group_size, part_rows.shape[0]) for part_rows in query_parts)
    )
    page_store = jnp.zeros((slots, PAGE_TOKENS, 2 * kv_width), jnp.bfloat16)
    key_piece = lax.all_gather(keys, "seq", axis=0, tiled=True)
    value_piece = lax.all_gather(values, "seq", axis=0, tiled=True)
    block_count = key_piece.shape[0] // shard_rows
    per_step = max(1, min(block_count, 512 // shard_rows))
    while block_count % per_step:
        per_step -= 1
    step_rows = per_step * shard_rows
    steps_count = block_count // per_step
    key_blocks = key_piece.reshape(steps_count, step_rows, kv_width)
    value_blocks = value_piece.reshape(steps_count, step_rows, kv_width)

    def one_block(inner_carry, block_item):
        block_states, stored = inner_carry
        key_block, value_block, number = block_item
        block_start = number * step_rows
        updated = []
        for query_state, query_block, query_pos in zip(block_states, shaped, positions):
            needed = block_start <= jnp.minimum(query_pos[-1], prompt_end - 1)
            updated.append(
                lax.cond(
                    needed,
                    lambda kept: attend_block(
                        kept,
                        query_block,
                        query_pos,
                        key_block,
                        value_block,
                        block_start,
                        prompt_end,
                    ),
                    lambda kept: kept,
                    query_state,
                )
            )
        stored = place_pages(
            stored, key_block, value_block, block_start, prompt_end, page_index, present
        )
        return ((tuple(updated), stored), None)

    result, unused = lax.scan(
        one_block,
        (states, page_store),
        (key_blocks, value_blocks, jnp.arange(steps_count, dtype=jnp.int32)),
    )
    final_states, stored = result
    outputs = [
        finish(query_state, query_pos, prompt_end)
        for query_state, query_pos in zip(final_states, positions)
    ]
    attended = outputs[0]
    return (attended, stored)


def solution(mesh):
    return jax.shard_map(
        local,
        mesh=mesh,
        in_specs=(
            P(("groups", "seq"), "head"),
            P(("groups", "seq"), "head"),
            P(("groups", "seq"), "head"),
            P("groups"),
            P("groups", None),
        ),
        out_specs=(P(("groups", "seq"), "head"), P(("groups", "seq"), None, "head")),
        check_vma=False,
    )
```

profile of v0, /device:TPU:26, one launch (start us, length us, event | category | flops | bytes accessed | tf_op | source)
XLA Modules:
  0.0 76.9 jit_solution(3035175965505265752)
XLA Ops:
  2.7 0.8 copy.34
  4.0 16.3 %all_gather.6 = bf16[1024,256]{1,0:T(8,128)(2,1)} all-gather(bf16[256,256]{1,0:T(8,128)(2,1)} %param.10), channel_id=1, replica_groups=mesh['groups'=2,'seq'=4,'head'=4] {'seq'}, dimensions={0}, use_global_device_ids=true | all-gather | bytes 655360 | tf_op jit(solution)/shard_map/all_gather | solution.py:118
  20.3 16.4 %all_gather.7 = bf16[1024,256]{1,0:T(8,128)(2,1)} all-gather(bf16[256,256]{1,0:T(8,128)(2,1)} %param.11), channel_id=1, replica_groups=mesh['groups'=2,'seq'=4,'head'=4] {'seq'}, dimensions={0}, use_global_device_ids=true | all-gather | bytes 655360 | tf_op jit(solution)/shard_map/all_gather | solution.py:119
  36.7 1.5 %copy.33 = bf16[256,2048]{0,1:T(8,128)(2,1)S(1)} copy(bf16[256,2048]{1,0:T(8,128)(2,1)} %param.9) | data formatting | bytes 2097152 | tf_op args[0]
  38.9 1.6 %broadcast_in_dim.106 = f32[2,8,256,128]{3,2,1,0:T(8,128)} broadcast(f32[]{:T(128)} %constant.102.clone.1), dimensions={} | broadcast | bytes 2097156 | tf_op jit(solution)/shard_map/broadcast_in_dim | solution.py:16
  40.4 31.5 %while.20 = (s32[]{:T(128)}, f32[2,8,256]{2,1,0:T(8,128)S(1)}, f32[2,8,256]{2,1,0:T(8,128)S(1)}, f32[2,8,256,128]{3,2,1,0:T(8,128)}, bf16[4,128,512]{1,2,0:T(8,1...) while((s32[]{:T(128)}, f32[2,8,256]{2,1,0:T(8,128)S(1)}, ...), condition=%wide.region_8.9_spmd.clone, body=%wide.region_3.8_spmd.clone.sunk | while | flops 1103377152 | bytes 57424572 | solution.py:157
  42.5 1.1 %constant_dynamic-slice_fusion.3 = (bf16[1,512,256]{2,1,0:T(8,128)(2,1)S(1)}, bf16[1,512,256]{2,1,0:T(8,128)(2,1)S(1)}) fusion(bf16[2,512,256]{2,1,0:T(8,128)(2,1)} %get-tuple-element.556, s32[]{:T(128)S(6)} %copy.67, bf16[2,512,256]{2,1,0:T(8,128)(2,1)} %get-tuple-element.555), kind=kLoop, calls=%fused_computation.31.clone.1 | loop fusion | bytes 1048580 | tf_op jit(solution)/shard_map/while/body/jit(dynamic_index_in_dim)/dynamic_slice | solution.py:157
  43.8 1.1 %broadcast_select_fusion.4 = (bf16[4,128,2,1,128]{4,2,1,0,3:T(2,128)(2,1)S(1)}, bf16[4,128,2,1,128]{4,2,1,0,3:T(2,128)(2,1)S(1)}) fusion(bf16[4,128,2,1,128]{4,2,1,0,3:T(2,128)(2,1)S(1)} %squeeze.31, pred[4,128]{1,0:T(4,128)(4,1)S(1)} %add_compare_fusion.2, bf16[4,128,2,1,128]{4,2,1,0,3:T(2,128)(2,1)S(1)} %squeeze.32), kind=kLoop, calls=%fused_computation.25.clone.1 | loop fusion | flops 262144 | bytes 1049088 | tf_op jit(solution)/shard_map/while/body/eval_jaxpr/jit(_where)/select_n | solution.py:86
  44.9 0.7 pad_maximum_fusion.2
  46.9 9.3 %conditional.3 = ((f32[2,8,256]{2,1,0:T(8,128)S(1)}, f32[2,8,256]{2,1,0:T(8,128)S(1)}, f32[2,8,256,128]{3,2,1,0:T(8,128)})) conditional(s32[]{:T(128)} %convert_element_type.41, (f32[2,8,256]{2,1,0:T(8,128)S(1)}, f32[2,8,256]{2,1,0:T(8,128)S(1)}, f32[2,8,256,128]{3,2,1,0:T(8,128)}) %tuple.62, (s32[]{:T(128)}, s32[]{:T(128)}, s32[]{:T(128)}, ...), branch_computations={%region_4.4_spmd, %region_5.7_spmd} | conditional | flops 1102325504 | bytes 49553512 | solution.py:137
  48.0 1.4 %fusion.2 = (f32[2,8,256]{2,1,0:T(8,128)S(1)}, f32[2,512,256,8]{2,1,3,0:T(8,128)S(1)}) fusion(pred[256,512]{0,1:T(8,128)(4,1)S(1)} %compare_and_fusion, bf16[256,2,8,128]{3,0,2,1:T(8,128)(2,1)S(1)} %get-tuple-element.235, bf16[512,2,128,1]{2,1,0,3:T(2,128)(2,1)S(1)} %bitcast.45), kind=kOutput, calls=%fused_computation.4 | convolution fusion | flops 543158272 | bytes 9846784 | tf_op jit(solution)/shard_map/while/body/eval_jaxpr/cond/branch_1_fun/rkgd,pkd->kgrp/dot_general | solution.py:27
  49.4 2.0 %fusion.4 = f32[2,8,256]{2,1,0:T(8,128)S(1)} fusion(f32[2,512,256,8]{2,1,3,0:T(8,128)S(1)} %get-tuple-element.398, f32[2,8,256]{2,1,0:T(8,128)S(1)} %max.6, pred[256,512]{0,1:T(8,128)(4,1)S(1)} %compare_and_fusion), kind=kLoop, calls=%fused_computation.6 | loop fusion | flops 10481664 | bytes 8552448 | tf_op jit(solution)/shard_map/while/body/eval_jaxpr/cond/branch_1_fun/reduce_sum | solution.py:38
  51.4 3.4 %multiply_add_fusion = f32[2,8,256,128]{3,2,1,0:T(8,128)S(1)} fusion(f32[2,8,256,128]{3,2,1,0:T(8,128)S(1)} %copy-done, f32[2,512,256,8]{2,1,3,0:T(8,128)S(1)} %get-tuple-element.398, f32[2,8,256]{2,1,0:T(8,128)S(1)} %max.6, pred[256,512]{0,1:T(8,128)(4,1)S(1)} %compare_and_fusion, f32[2,8,256]{2,1,0:T(8,128)S(1)} %get-tuple-element.396, ...), kind=kOutput, calls=%fused_computation.9 | convolution fusion | flops 548405248 | bytes 13008896 | tf_op jit(solution)/shard_map/while/body/eval_jaxpr/cond/branch_1_fun/kgrp,pkd->kgrd/dot_general | solution.py:39
  54.9 1.3 %copy-done.1 = f32[2,8,256,128]{3,2,1,0:T(8,128)} copy-done((f32[2,8,256,128]{3,2,1,0:T(8,128)}, f32[2,8,256,128]{3,2,1,0:T(8,128)S(1)}, u32[]{:S(2)}) %copy-start.1) | copy-done | bytes 2097176 | tf_op jit(solution)/shard_map/while/body/eval_jaxpr/cond
  58.3 1.1 %constant_dynamic-slice_fusion.3 = (bf16[1,512,256]{2,1,0:T(8,128)(2,1)S(1)}, bf16[1,512,256]{2,1,0:T(8,128)(2,1)S(1)}) fusion(bf16[2,512,256]{2,1,0:T(8,128)(2,1)} %get-tuple-element.556, s32[]{:T(128)S(6)} %copy.67, bf16[2,512,256]{2,1,0:T(8,128)(2,1)} %get-tuple-element.555), kind=kLoop, calls=%fused_computation.31.clone.1 | loop fusion | bytes 1048580 | tf_op jit(solution)/shard_map/while/body/jit(dynamic_index_in_dim)/dynamic_slice | solution.py:157
  59.5 1.1 %broadcast_select_fusion.4 = (bf16[4,128,2,1,128]{4,2,1,0,3:T(2,128)(2,1)S(1)}, bf16[4,128,2,1,128]{4,2,1,0,3:T(2,128)(2,1)S(1)}) fusion(bf16[4,128,2,1,128]{4,2,1,0,3:T(2,128)(2,1)S(1)} %squeeze.31, pred[4,128]{1,0:T(4,128)(4,1)S(1)} %add_compare_fusion.2, bf16[4,128,2,1,128]{4,2,1,0,3:T(2,128)(2,1)S(1)} %squeeze.32), kind=kLoop, calls=%fused_computation.25.clone.1 | loop fusion | flops 262144 | bytes 1049088 | tf_op jit(solution)/shard_map/while/body/eval_jaxpr/jit(_where)/select_n | solution.py:86
  62.7 9.3 %conditional.3 = ((f32[2,8,256]{2,1,0:T(8,128)S(1)}, f32[2,8,256]{2,1,0:T(8,128)S(1)}, f32[2,8,256,128]{3,2,1,0:T(8,128)})) conditional(s32[]{:T(128)} %convert_element_type.41, (f32[2,8,256]{2,1,0:T(8,128)S(1)}, f32[2,8,256]{2,1,0:T(8,128)S(1)}, f32[2,8,256,128]{3,2,1,0:T(8,128)}) %tuple.62, (s32[]{:T(128)}, s32[]{:T(128)}, s32[]{:T(128)}, ...), branch_computations={%region_4.4_spmd, %region_5.7_spmd} | conditional | flops 1102325504 | bytes 49553512 | solution.py:137
  63.7 1.4 %fusion.2 = (f32[2,8,256]{2,1,0:T(8,128)S(1)}, f32[2,512,256,8]{2,1,3,0:T(8,128)S(1)}) fusion(pred[256,512]{0,1:T(8,128)(4,1)S(1)} %compare_and_fusion, bf16[256,2,8,128]{3,0,2,1:T(8,128)(2,1)S(1)} %get-tuple-element.235, bf16[512,2,128,1]{2,1,0,3:T(2,128)(2,1)S(1)} %bitcast.45), kind=kOutput, calls=%fused_computation.4 | convolution fusion | flops 543158272 | bytes 9846784 | tf_op jit(solution)/shard_map/while/body/eval_jaxpr/cond/branch_1_fun/rkgd,pkd->kgrp/dot_general | solution.py:27
  65.2 2.0 %fusion.4 = f32[2,8,256]{2,1,0:T(8,128)S(1)} fusion(f32[2,512,256,8]{2,1,3,0:T(8,128)S(1)} %get-tuple-element.398, f32[2,8,256]{2,1,0:T(8,128)S(1)} %max.6, pred[256,512]{0,1:T(8,128)(4,1)S(1)} %compare_and_fusion), kind=kLoop, calls=%fused_computation.6 | loop fusion | flops 10481664 | bytes 8552448 | tf_op jit(solution)/shard_map/while/body/eval_jaxpr/cond/branch_1_fun/reduce_sum | solution.py:38
  67.2 3.4 %multiply_add_fusion = f32[2,8,256,128]{3,2,1,0:T(8,128)S(1)} fusion(f32[2,8,256,128]{3,2,1,0:T(8,128)S(1)} %copy-done, f32[2,512,256,8]{2,1,3,0:T(8,128)S(1)} %get-tuple-element.398, f32[2,8,256]{2,1,0:T(8,128)S(1)} %max.6, pred[256,512]{0,1:T(8,128)(4,1)S(1)} %compare_and_fusion, f32[2,8,256]{2,1,0:T(8,128)S(1)} %get-tuple-element.396, ...), kind=kOutput, calls=%fused_computation.9 | convolution fusion | flops 548405248 | bytes 13008896 | tf_op jit(solution)/shard_map/while/body/eval_jaxpr/cond/branch_1_fun/kgrp,pkd->kgrd/dot_general | solution.py:39
  70.6 1.3 %copy-done.1 = f32[2,8,256,128]{3,2,1,0:T(8,128)} copy-done((f32[2,8,256,128]{3,2,1,0:T(8,128)}, f32[2,8,256,128]{3,2,1,0:T(8,128)S(1)}, u32[]{:S(2)}) %copy-start.1) | copy-done | bytes 2097176 | tf_op jit(solution)/shard_map/while/body/eval_jaxpr/cond
  72.0 2.0 %fusion.17 = bf16[256,2,8,128]{3,0,2,1:T(8,128)(2,1)S(1)} fusion(f32[2,8,256,128]{3,2,1,0:T(8,128)} %get-tuple-element.262, f32[2,8,256]{2,1,0:T(8,128)S(1)} %broadcast_select_fusion.2, pred[256]{0:T(512)(128)(4,1)S(1)} %broadcast_compare_fusion.1), kind=kLoop, calls=%fused_computation.35 | loop fusion | flops 1572864 | bytes 3162368 | tf_op jit(solution)/shard_map/convert_element_type | solution.py:53
  74.7 1.2 %copy.53 = bf16[32,8,16,128]{3,1,2,0:T(8,128)(2,1)} copy(bf16[32,8,16,128]{3,2,1,0:T(8,128)(2,1)S(1)} %bitcast.47) | data formatting | bytes 2097152
  75.9 1.0 %copy.37 = bf16[4,128,512]{2,1,0:T(8,128)(2,1)} copy(bf16[4,128,512]{1,2,0:T(8,128)(2,1)S(1)} %get-tuple-element.363) | data formatting | bytes 1048576
  (62 shorter events, 10.8 us)
Async XLA Ops:
  47.9 3.5 %copy-start = (f32[2,8,256,128]{3,2,1,0:T(8,128)S(1)}, f32[2,8,256,128]{3,2,1,0:T(8,128)}, u32[]{:S(2)}) copy-start(f32[2,8,256,128]{3,2,1,0:T(8,128)} %get-tuple-element.237) | copy-start | bytes 6291460 | tf_op jit(solution)/shard_map/while/body/eval_jaxpr/cond
  54.8 1.4 %copy-start.1 = (f32[2,8,256,128]{3,2,1,0:T(8,128)}, f32[2,8,256,128]{3,2,1,0:T(8,128)S(1)}, u32[]{:S(2)}) copy-start(f32[2,8,256,128]{3,2,1,0:T(8,128)S(1)} %multiply_add_fusion) | copy-start | bytes 6291460 | tf_op jit(solution)/shard_map/while/body/eval_jaxpr/cond
  63.7 3.5 %copy-start = (f32[2,8,256,128]{3,2,1,0:T(8,128)S(1)}, f32[2,8,256,128]{3,2,1,0:T(8,128)}, u32[]{:S(2)}) copy-start(f32[2,8,256,128]{3,2,1,0:T(8,128)} %get-tuple-element.237) | copy-start | bytes 6291460 | tf_op jit(solution)/shard_map/while/body/eval_jaxpr/cond
  70.6 1.4 %copy-start.1 = (f32[2,8,256,128]{3,2,1,0:T(8,128)}, f32[2,8,256,128]{3,2,1,0:T(8,128)S(1)}, u32[]{:S(2)}) copy-start(f32[2,8,256,128]{3,2,1,0:T(8,128)S(1)} %multiply_add_fusion) | copy-start | bytes 6291460 | tf_op jit(solution)/shard_map/while/body/eval_jaxpr/cond
where the time goes:
time: 77.3 us; the launch traced here: 76.9 us
  blocking collectives  32.7 us (42%)
  local copies, waits for them, and re-layouts  17.1 us (22%)
  other arithmetic  13.6 us (18%)
  matrix products  9.64 us (12%)
  between operations  2.06 us (3%)
  loops' own time  1.84 us (2%)
    all_gather x1, blocking collectives, local(): value_piece = lax.all_gather(values, 'seq', axis=0, tiled=True)  16.4 us
    all_gather x1, blocking collectives, local(): key_piece = lax.all_gather(keys, 'seq', axis=0, tiled=True)  16.3 us
    dot_general x2, matrix products, attend_block(): jnp.einsum('kgrp,pkd->kgrd', weights.astype(jnp.bfloat16), values_split,...  6.81 us
    unnamed x5, local copies, waits for them, and re-layouts  5.16 us
    reduce_sum x2, other arithmetic, attend_block(): denominator = query_state[1] * factor + jnp.sum(weights, axis=-1)  4.01 us
    dynamic_slice x4, local copies, waits for them, and re-layouts, local(): lax.scan(one_block, (states, page_store), (key_blocks, value_blocks, jnp....  3.47 us
    dot_general x2, matrix products, attend_block(): jnp.einsum('rkgd,pkd->kgrp', query_block, keys_split, preferred_element_t...  2.83 us
    cond x10, local copies, waits for them, and re-layouts  2.71 us

commit v1 on v0

--- a/solution.py
+++ b/solution.py
@@ -116,7 +116,12 @@
     )
     page_store = jnp.zeros((slots, PAGE_TOKENS, 2 * kv_width), jnp.bfloat16)
     key_piece = lax.all_gather(keys, "seq", axis=0, tiled=True)
-    value_piece = lax.all_gather(values, "seq", axis=0, tiled=True)
+    ring = [values]
+    for hop in range(3):
+        ring.append(lax.ppermute(ring[-1], "seq", [(dev, (dev + 1) % 4) for dev in range(4)]))
+    value_piece = jnp.roll(
+        jnp.concatenate(ring[::-1], axis=0), (lax.axis_index("seq") + 1) * ring[0].shape[0], axis=0
+    )
     block_count = key_piece.shape[0] // shard_rows
     per_step = max(1, min(block_count, 512 // shard_rows))
     while block_count % per_step:

time: 77.3 us -> 71.3 us (0.922)
  blocking collectives: 32.7 us -> 16.9 us
  waiting for transfers between devices: 0 us -> 3.76 us
  starting transfers between devices: 0 us -> 3.55 us
  local copies, waits for them, and re-layouts: 17.1 us -> 19.7 us
    all_gather x1 -> x0, blocking collectives: 16.4 us -> none  [local(): value_piece = lax.all_gather(values, 'seq', axis=0, tiled=True)]
    ppermute x0 -> x3, waiting for transfers between devices: none -> 3.76 us  [local(): lax.ppermute(ring[-1], 'seq', [(dev, (dev + 1) % 4) for dev in range(4)])]
    ppermute x0 -> x3, starting transfers between devices: none -> 3.55 us  [local(): lax.ppermute(ring[-1], 'seq', [(dev, (dev + 1) % 4) for dev in range(4)])]
    unnamed x5 -> x12, local copies, waits for them, and re-layouts: 5.16 us -> 6.13 us
    concatenate x0 -> x1, local copies, waits for them, and re-layouts: none -> 0.92 us  [local(): jnp.roll(jnp.concatenate(ring[::-1], axis=0), (lax.axis_index('seq') + 1)...]
    dynamic_slice x0 -> x1, local copies, waits for them, and re-layouts: none -> 0.84 us  [local(): jnp.roll(jnp.concatenate(ring[::-1], axis=0), (lax.axis_index('seq') + 1)...]
  transfers between devices with their start and end apart: 0 -> 3, of which waited for: 0 -> 1; matrix products, arithmetic and copies ran while one was open for 0% -> 6% of each run, Pallas kernels for 0% -> 0%
where the time goes in v1:
time: 71.3 us; the launch traced here: 70.9 us
  local copies, waits for them, and re-layouts  19.7 us (28%)
  blocking collectives  16.9 us (24%)
  other arithmetic  13.6 us (19%)
  matrix products  9.64 us (14%)
  waiting for transfers between devices  3.76 us (5%)
  starting transfers between devices  3.55 us (5%)
  between operations  2.04 us (3%)
  loops' own time  1.81 us (3%)
    all_gather x1, blocking collectives, local(): key_piece = lax.all_gather(keys, 'seq', axis=0, tiled=True)  16.9 us
    dot_general x2, matrix products, attend_block(): jnp.einsum('kgrp,pkd->kgrd', weights.astype(jnp.bfloat16), values_split,...  6.8 us
    unnamed x12, local copies, waits for them, and re-layouts  6.13 us
    reduce_sum x2, other arithmetic, attend_block(): denominator = query_state[1] * factor + jnp.sum(weights, axis=-1)  4.01 us
    ppermute x3, waiting for transfers between devices, local(): lax.ppermute(ring[-1], 'seq', [(dev, (dev + 1) % 4) for dev in range(4)])  3.76 us
    ppermute x3, starting transfers between devices, local(): lax.ppermute(ring[-1], 'seq', [(dev, (dev + 1) % 4) for dev in range(4)])  3.55 us
    dynamic_slice x4, local copies, waits for them, and re-layouts, local(): lax.scan(one_block, (states, page_store), (key_blocks, value_blocks, jnp....  3.43 us
    dot_general x2, matrix products, attend_block(): jnp.einsum('rkgd,pkd->kgrp', query_block, keys_split, preferred_element_t...  2.83 us
  transfers between devices with their start and end apart: 3, of which 1 were waited for; matrix products, arithmetic and copies ran while one was open for 6% of the time, Pallas kernels for 0%

profile of v1, /device:TPU:26, one launch (start us, length us, event | category | flops | bytes accessed | tf_op | source)
XLA Modules:
  0.0 70.9 jit_solution(614954022146319595)
XLA Ops:
  1.8 16.9 %all_gather.3 = bf16[1024,256]{1,0:T(8,128)(2,1)} all-gather(bf16[256,256]{1,0:T(8,128)(2,1)} %param.10), channel_id=1, replica_groups=mesh['groups'=2,'seq'=4,'head'=4] {'seq'}, dimensions={0}, use_global_device_ids=true | all-gather | bytes 655360 | tf_op jit(solution)/shard_map/all_gather | solution.py:118
  18.8 1.0 %collective-permute-start.1 = (bf16[256,256]{1,0:T(8,128)(2,1)S(1)}, bf16[256,256]{1,0:T(8,128)(2,1)S(1)}, u32[]{:S(2)}, u32[]{:S(2)}) collective-permute-start(bf16[256,256]{1,0:T(8,128)(2,1)S(1)} %collective-permute-done), channel_id=1, source_target_pairs={{0,4},{4,8},{8,12},{12,0},{1,5},{5,9},{9,13},{13,1},{2,6},{6,10},{... | collective-permute-start | bytes 393224 | tf_op jit(solution)/shard_map/ppermute | solution.py:121
  20.6 3.8 %collective-permute-done.1 = bf16[256,256]{1,0:T(8,128)(2,1)S(1)} collective-permute-done((bf16[256,256]{1,0:T(8,128)(2,1)S(1)}, bf16[256,256]{1,0:T(8,128)(2,1)S(1)}, u32[]{:S(2)}, u32[]{:S(2)}) %collective-permute-start.1) | collective-permute-done | bytes 131104 | tf_op jit(solution)/shard_map/ppermute | solution.py:121
  24.4 2.2 %collective-permute-start.2 = (bf16[256,256]{1,0:T(8,128)(2,1)S(1)}, bf16[256,256]{1,0:T(8,128)(2,1)S(1)}, u32[]{:S(2)}, u32[]{:S(2)}) collective-permute-start(bf16[256,256]{1,0:T(8,128)(2,1)S(1)} %collective-permute-done.1), channel_id=1, source_target_pairs={{0,4},{4,8},{8,12},{12,0},{1,5},{5,9},{9,13},{13,1},{2,6},{6,10},{... | collective-permute-start | bytes 393224 | tf_op jit(solution)/shard_map/ppermute | solution.py:121
  27.2 1.5 %copy.33 = bf16[256,2048]{0,1:T(8,128)(2,1)S(1)} copy(bf16[256,2048]{1,0:T(8,128)(2,1)} %param.9) | data formatting | bytes 2097152 | tf_op args[0]
  32.9 1.6 %broadcast_in_dim.106 = f32[2,8,256,128]{3,2,1,0:T(8,128)} broadcast(f32[]{:T(128)} %constant.121.clone.1), dimensions={} | broadcast | bytes 2097156 | tf_op jit(solution)/shard_map/broadcast_in_dim | solution.py:16
  34.5 31.4 %while.20 = (s32[]{:T(128)}, f32[2,8,256]{2,1,0:T(8,128)S(1)}, f32[2,8,256]{2,1,0:T(8,128)S(1)}, f32[2,8,256,128]{3,2,1,0:T(8,128)}, bf16[4,128,512]{1,2,0:T(8,1...) while((s32[]{:T(128)}, f32[2,8,256]{2,1,0:T(8,128)S(1)}, ...), condition=%wide.region_8.9_spmd.clone, body=%wide.region_3.8_spmd.clone.sunk | while | flops 1103377152 | bytes 57424572 | solution.py:162
  36.6 1.1 %constant_dynamic-slice_fusion.4 = (bf16[1,512,256]{2,1,0:T(8,128)(2,1)S(1)}, bf16[1,512,256]{2,1,0:T(8,128)(2,1)S(1)}) fusion(bf16[2,512,256]{2,1,0:T(8,128)(2,1)} %get-tuple-element.556, s32[]{:T(128)S(6)} %copy.74, bf16[2,512,256]{2,1,0:T(8,128)(2,1)} %get-tuple-element.555), kind=kLoop, calls=%fused_computation.31.clone.1 | loop fusion | bytes 1048580 | tf_op jit(solution)/shard_map/while/body/jit(dynamic_index_in_dim)/dynamic_slice | solution.py:162
  37.8 1.1 %broadcast_select_fusion.4 = (bf16[4,128,2,1,128]{4,2,1,0,3:T(2,128)(2,1)S(1)}, bf16[4,128,2,1,128]{4,2,1,0,3:T(2,128)(2,1)S(1)}) fusion(bf16[4,128,2,1,128]{4,2,1,0,3:T(2,128)(2,1)S(1)} %squeeze.31, pred[4,128]{1,0:T(4,128)(4,1)S(1)} %add_compare_fusion.2, bf16[4,128,2,1,128]{4,2,1,0,3:T(2,128)(2,1)S(1)} %squeeze.32), kind=kLoop, calls=%fused_computation.25.clone.1 | loop fusion | flops 262144 | bytes 1049088 | tf_op jit(solution)/shard_map/while/body/eval_jaxpr/jit(_where)/select_n | solution.py:86
  40.9 9.3 %conditional.3 = ((f32[2,8,256]{2,1,0:T(8,128)S(1)}, f32[2,8,256]{2,1,0:T(8,128)S(1)}, f32[2,8,256,128]{3,2,1,0:T(8,128)})) conditional(s32[]{:T(128)} %convert_element_type.41, (f32[2,8,256]{2,1,0:T(8,128)S(1)}, f32[2,8,256]{2,1,0:T(8,128)S(1)}, f32[2,8,256,128]{3,2,1,0:T(8,128)}) %tuple.62, (s32[]{:T(128)}, s32[]{:T(128)}, s32[]{:T(128)}, ...), branch_computations={%region_4.4_spmd, %region_5.7_spmd} | conditional | flops 1102325504 | bytes 49553512 | solution.py:142
  42.0 1.4 %fusion.2 = (f32[2,8,256]{2,1,0:T(8,128)S(1)}, f32[2,512,256,8]{2,1,3,0:T(8,128)S(1)}) fusion(pred[256,512]{0,1:T(8,128)(4,1)S(1)} %compare_and_fusion, bf16[256,2,8,128]{3,0,2,1:T(8,128)(2,1)S(1)} %get-tuple-element.235, bf16[512,2,128,1]{2,1,0,3:T(2,128)(2,1)S(1)} %bitcast.45), kind=kOutput, calls=%fused_computation.4 | convolution fusion | flops 543158272 | bytes 9846784 | tf_op jit(solution)/shard_map/while/body/eval_jaxpr/cond/branch_1_fun/rkgd,pkd->kgrp/dot_general | solution.py:27
  43.4 2.0 %fusion.4 = f32[2,8,256]{2,1,0:T(8,128)S(1)} fusion(f32[2,512,256,8]{2,1,3,0:T(8,128)S(1)} %get-tuple-element.398, f32[2,8,256]{2,1,0:T(8,128)S(1)} %max.6, pred[256,512]{0,1:T(8,128)(4,1)S(1)} %compare_and_fusion), kind=kLoop, calls=%fused_computation.6 | loop fusion | flops 10481664 | bytes 8552448 | tf_op jit(solution)/shard_map/while/body/eval_jaxpr/cond/branch_1_fun/reduce_sum | solution.py:38
  45.5 3.4 %multiply_add_fusion = f32[2,8,256,128]{3,2,1,0:T(8,128)S(1)} fusion(f32[2,8,256,128]{3,2,1,0:T(8,128)S(1)} %copy-done, f32[2,512,256,8]{2,1,3,0:T(8,128)S(1)} %get-tuple-element.398, f32[2,8,256]{2,1,0:T(8,128)S(1)} %max.6, pred[256,512]{0,1:T(8,128)(4,1)S(1)} %compare_and_fusion, f32[2,8,256]{2,1,0:T(8,128)S(1)} %get-tuple-element.396, ...), kind=kOutput, calls=%fused_computation.9 | convolution fusion | flops 548405248 | bytes 13008896 | tf_op jit(solution)/shard_map/while/body/eval_jaxpr/cond/branch_1_fun/kgrp,pkd->kgrd/dot_general | solution.py:39
  48.9 1.3 %copy-done.1 = f32[2,8,256,128]{3,2,1,0:T(8,128)} copy-done((f32[2,8,256,128]{3,2,1,0:T(8,128)}, f32[2,8,256,128]{3,2,1,0:T(8,128)S(1)}, u32[]{:S(2)}) %copy-start.1) | copy-done | bytes 2097176 | tf_op jit(solution)/shard_map/while/body/eval_jaxpr/cond
  52.3 1.1 %constant_dynamic-slice_fusion.4 = (bf16[1,512,256]{2,1,0:T(8,128)(2,1)S(1)}, bf16[1,512,256]{2,1,0:T(8,128)(2,1)S(1)}) fusion(bf16[2,512,256]{2,1,0:T(8,128)(2,1)} %get-tuple-element.556, s32[]{:T(128)S(6)} %copy.74, bf16[2,512,256]{2,1,0:T(8,128)(2,1)} %get-tuple-element.555), kind=kLoop, calls=%fused_computation.31.clone.1 | loop fusion | bytes 1048580 | tf_op jit(solution)/shard_map/while/body/jit(dynamic_index_in_dim)/dynamic_slice | solution.py:162
  53.5 1.1 %broadcast_select_fusion.4 = (bf16[4,128,2,1,128]{4,2,1,0,3:T(2,128)(2,1)S(1)}, bf16[4,128,2,1,128]{4,2,1,0,3:T(2,128)(2,1)S(1)}) fusion(bf16[4,128,2,1,128]{4,2,1,0,3:T(2,128)(2,1)S(1)} %squeeze.31, pred[4,128]{1,0:T(4,128)(4,1)S(1)} %add_compare_fusion.2, bf16[4,128,2,1,128]{4,2,1,0,3:T(2,128)(2,1)S(1)} %squeeze.32), kind=kLoop, calls=%fused_computation.25.clone.1 | loop fusion | flops 262144 | bytes 1049088 | tf_op jit(solution)/shard_map/while/body/eval_jaxpr/jit(_where)/select_n | solution.py:86
  56.6 9.3 %conditional.3 = ((f32[2,8,256]{2,1,0:T(8,128)S(1)}, f32[2,8,256]{2,1,0:T(8,128)S(1)}, f32[2,8,256,128]{3,2,1,0:T(8,128)})) conditional(s32[]{:T(128)} %convert_element_type.41, (f32[2,8,256]{2,1,0:T(8,128)S(1)}, f32[2,8,256]{2,1,0:T(8,128)S(1)}, f32[2,8,256,128]{3,2,1,0:T(8,128)}) %tuple.62, (s32[]{:T(128)}, s32[]{:T(128)}, s32[]{:T(128)}, ...), branch_computations={%region_4.4_spmd, %region_5.7_spmd} | conditional | flops 1102325504 | bytes 49553512 | solution.py:142
  57.7 1.4 %fusion.2 = (f32[2,8,256]{2,1,0:T(8,128)S(1)}, f32[2,512,256,8]{2,1,3,0:T(8,128)S(1)}) fusion(pred[256,512]{0,1:T(8,128)(4,1)S(1)} %compare_and_fusion, bf16[256,2,8,128]{3,0,2,1:T(8,128)(2,1)S(1)} %get-tuple-element.235, bf16[512,2,128,1]{2,1,0,3:T(2,128)(2,1)S(1)} %bitcast.45), kind=kOutput, calls=%fused_computation.4 | convolution fusion | flops 543158272 | bytes 9846784 | tf_op jit(solution)/shard_map/while/body/eval_jaxpr/cond/branch_1_fun/rkgd,pkd->kgrp/dot_general | solution.py:27
  59.1 2.0 %fusion.4 = f32[2,8,256]{2,1,0:T(8,128)S(1)} fusion(f32[2,512,256,8]{2,1,3,0:T(8,128)S(1)} %get-tuple-element.398, f32[2,8,256]{2,1,0:T(8,128)S(1)} %max.6, pred[256,512]{0,1:T(8,128)(4,1)S(1)} %compare_and_fusion), kind=kLoop, calls=%fused_computation.6 | loop fusion | flops 10481664 | bytes 8552448 | tf_op jit(solution)/shard_map/while/body/eval_jaxpr/cond/branch_1_fun/reduce_sum | solution.py:38
  61.2 3.4 %multiply_add_fusion = f32[2,8,256,128]{3,2,1,0:T(8,128)S(1)} fusion(f32[2,8,256,128]{3,2,1,0:T(8,128)S(1)} %copy-done, f32[2,512,256,8]{2,1,3,0:T(8,128)S(1)} %get-tuple-element.398, f32[2,8,256]{2,1,0:T(8,128)S(1)} %max.6, pred[256,512]{0,1:T(8,128)(4,1)S(1)} %compare_and_fusion, f32[2,8,256]{2,1,0:T(8,128)S(1)} %get-tuple-element.396, ...), kind=kOutput, calls=%fused_computation.9 | convolution fusion | flops 548405248 | bytes 13008896 | tf_op jit(solution)/shard_map/while/body/eval_jaxpr/cond/branch_1_fun/kgrp,pkd->kgrd/dot_general | solution.py:39
  64.6 1.3 %copy-done.1 = f32[2,8,256,128]{3,2,1,0:T(8,128)} copy-done((f32[2,8,256,128]{3,2,1,0:T(8,128)}, f32[2,8,256,128]{3,2,1,0:T(8,128)S(1)}, u32[]{:S(2)}) %copy-start.1) | copy-done | bytes 2097176 | tf_op jit(solution)/shard_map/while/body/eval_jaxpr/cond
  66.0 2.0 %fusion.17 = bf16[256,2,8,128]{3,0,2,1:T(8,128)(2,1)S(1)} fusion(f32[2,8,256,128]{3,2,1,0:T(8,128)} %get-tuple-element.262, f32[2,8,256]{2,1,0:T(8,128)S(1)} %broadcast_select_fusion.2, pred[256]{0:T(512)(128)(4,1)S(1)} %broadcast_compare_fusion.1), kind=kLoop, calls=%fused_computation.35 | loop fusion | flops 1572864 | bytes 3162368 | tf_op jit(solution)/shard_map/convert_element_type | solution.py:53
  68.7 1.2 %copy.53 = bf16[32,8,16,128]{3,1,2,0:T(8,128)(2,1)} copy(bf16[32,8,16,128]{3,2,1,0:T(8,128)(2,1)S(1)} %bitcast.47) | data formatting | bytes 2097152
  69.9 1.0 %copy.37 = bf16[4,128,512]{2,1,0:T(8,128)(2,1)} copy(bf16[4,128,512]{1,2,0:T(8,128)(2,1)S(1)} %get-tuple-element.363) | data formatting | bytes 1048576
  (76 shorter events, 15.2 us)
Async XLA Ops:
  0.6 18.2 %collective-permute-start = (bf16[256,256]{1,0:T(8,128)(2,1)}, bf16[256,256]{1,0:T(8,128)(2,1)S(1)}, u32[]{:S(2)}, u32[]{:S(2)}) collective-permute-start(bf16[256,256]{1,0:T(8,128)(2,1)} %param.11), channel_id=1, source_target_pairs={{0,4},{4,8},{8,12},{12,0},{1,5},{5,9},{9,13},{13,1},{2,6},{6,10},{... | collective-permute-start | bytes 393224 | tf_op jit(solution)/shard_map/ppermute | solution.py:121
  18.8 5.6 %collective-permute-start.1 = (bf16[256,256]{1,0:T(8,128)(2,1)S(1)}, bf16[256,256]{1,0:T(8,128)(2,1)S(1)}, u32[]{:S(2)}, u32[]{:S(2)}) collective-permute-start(bf16[256,256]{1,0:T(8,128)(2,1)S(1)} %collective-permute-done), channel_id=1, source_target_pairs={{0,4},{4,8},{8,12},{12,0},{1,5},{5,9},{9,13},{13,1},{2,6},{6,10},{... | collective-permute-start | bytes 393224 | tf_op jit(solution)/shard_map/ppermute | solution.py:121
  24.4 5.8 %collective-permute-start.2 = (bf16[256,256]{1,0:T(8,128)(2,1)S(1)}, bf16[256,256]{1,0:T(8,128)(2,1)S(1)}, u32[]{:S(2)}, u32[]{:S(2)}) collective-permute-start(bf16[256,256]{1,0:T(8,128)(2,1)S(1)} %collective-permute-done.1), channel_id=1, source_target_pairs={{0,4},{4,8},{8,12},{12,0},{1,5},{5,9},{9,13},{13,1},{2,6},{6,10},{... | collective-permute-start | bytes 393224 | tf_op jit(solution)/shard_map/ppermute | solution.py:121
  42.0 3.5 %copy-start = (f32[2,8,256,128]{3,2,1,0:T(8,128)S(1)}, f32[2,8,256,128]{3,2,1,0:T(8,128)}, u32[]{:S(2)}) copy-start(f32[2,8,256,128]{3,2,1,0:T(8,128)} %get-tuple-element.237) | copy-start | bytes 6291460 | tf_op jit(solution)/shard_map/while/body/eval_jaxpr/cond
  48.9 1.4 %copy-start.1 = (f32[2,8,256,128]{3,2,1,0:T(8,128)}, f32[2,8,256,128]{3,2,1,0:T(8,128)S(1)}, u32[]{:S(2)}) copy-start(f32[2,8,256,128]{3,2,1,0:T(8,128)S(1)} %multiply_add_fusion) | copy-start | bytes 6291460 | tf_op jit(solution)/shard_map/while/body/eval_jaxpr/cond
  57.7 3.5 %copy-start = (f32[2,8,256,128]{3,2,1,0:T(8,128)S(1)}, f32[2,8,256,128]{3,2,1,0:T(8,128)}, u32[]{:S(2)}) copy-start(f32[2,8,256,128]{3,2,1,0:T(8,128)} %get-tuple-element.237) | copy-start | bytes 6291460 | tf_op jit(solution)/shard_map/while/body/eval_jaxpr/cond
  64.6 1.4 %copy-start.1 = (f32[2,8,256,128]{3,2,1,0:T(8,128)}, f32[2,8,256,128]{3,2,1,0:T(8,128)S(1)}, u32[]{:S(2)}) copy-start(f32[2,8,256,128]{3,2,1,0:T(8,128)S(1)} %multiply_add_fusion) | copy-start | bytes 6291460 | tf_op jit(solution)/shard_map/while/body/eval_jaxpr/cond
